TPU v7x, 256 devices: a whole 4x4x8 slice. The times are simulated.
256 devices in a mesh: rows: 64 (over z, x, core), cols: 4 (over y).
Axes of the slice: x: 4, y: 4, z: 8, core: 2. Of those that a mesh axis runs over, the one named last changes fastest.
Arguments:
- tables: float32 [4, 32768, 512], P(None, 'rows', 'cols'), may hold values from -1.5 to 1.5
- dense_features: float32 [2048, 512], P('rows', 'cols'), may hold values from -6 to 6
- slot_rows: int32 [64, 64, 4, 64], P('rows'), may hold values from 0 to 511, as said below
- slot_examples: int32 [64, 64, 4, 64], P('rows'), may hold values from 0 to 31, as said below
- slot_counts: int32 [64, 64, 4], P('rows'), may hold values from 21 to 64, as said below
Outputs:
- pooled: float32 [2048, 4, 512], P('rows', None, 'cols')
- interactions: float32 [2048, 10], P('rows')
Inputs may be any that keep to these rules, and one draw needn't show every extreme that they name: slot_rows[s, o, t, c] names row o * 512 + value of table t. `slot_examples`: an example of the source device s. `slot_counts`: slots 0 to count - 1 of a bucket are live, the others unused; some bucket of every draw is full.
All inputs are finite; a program needn't handle non-finite values.
Results may differ from a plain program's by a relative error of at most 0.0003.
Values sent between devices are 32-bit elements; how exact they have to be, the bound alone decides.
A program may use at most 64 MiB of HBM per device.

v0:
```python
import math

import jax
import jax.numpy as jnp
from jax import lax
from jax.sharding import Mesh
from jax.sharding import PartitionSpec as P

E = 512
ROWS = ("rows_0", "rows_1", "rows_2")


def in_one_piece(arrays, axis, split_dim, concat_dim, along):
    widths = [math.prod(a.shape[along:]) for a in arrays]
    both = jnp.concatenate(
        [a.reshape(*a.shape[:along], w) for a, w in zip(arrays, widths)], axis=along
    )
    filled = lax.all_to_all(both, axis, split_axis=split_dim, concat_axis=concat_dim, tiled=True)
    tiles = jnp.split(filled, [sum(widths[:k]) for k in range(1, len(widths))], axis=along)
    return tuple(
        (b.reshape(*filled.shape[:along], *a.shape[along:]) for a, b in zip(arrays, tiles))
    )


def in_blocks(x, dim, size):
    before, after = (x.shape[:dim], x.shape[dim + 1 :])
    return jnp.moveaxis(x.reshape(*before, size, -1, *after), dim, 0)


def sent_and_summed(x, axis, dim):
    size = lax.axis_size(axis)
    tiles = lax.all_to_all(in_blocks(x, dim, size), axis, 0, 0, tiled=True)
    return jnp.sum(tiles, axis=0)


def sum_by_axis(x, axes, dim):
    far, near = axes
    tiles = in_blocks(x, dim, lax.axis_size(far))
    nearer = sent_and_summed(tiles, near, dim + 1)
    arrived = lax.all_to_all(nearer, far, split_axis=0, concat_axis=0, tiled=True)
    return arrived.sum(axis=0)


def copy_for_each(x, axis):
    copies = jnp.broadcast_to(x, (lax.axis_size(axis), *x.shape))
    return lax.all_to_all(copies, axis, split_axis=0, concat_axis=0, tiled=True)


def over_copies(x, axis):
    return copy_for_each(x, axis).sum(axis=0)


def lookup(got_rows, tables):
    range_rows = tables.shape[1]
    row_ids = jnp.arange(range_rows, dtype=jnp.int32)

    def one_table(pieces):
        rows_table, table_slice = pieces
        selector = (rows_table[:, :, None] == row_ids[None, None, :]).astype(jnp.float32)
        return jnp.einsum("scr,re->sce", selector, table_slice, precision=lax.Precision.HIGHEST)

    picked = lax.map(one_table, (jnp.moveaxis(got_rows, 1, 0), tables))
    return jnp.moveaxis(picked, 0, 1)


def upper_pairs(gram_matrix, count):
    pieces = [gram_matrix[:, first, first + 1 :] for first in range(count - 1)]
    return jnp.concatenate(pieces, axis=1)


def body(tables, dense_features, slot_rows, slot_examples, slot_counts):
    table_count = tables.shape[0]
    width = tables.shape[2]
    capacity = slot_rows.shape[3]
    examples_here = dense_features.shape[0]
    slot_index = jnp.arange(capacity, dtype=jnp.int32)
    example_ids = jnp.arange(examples_here, dtype=jnp.int32)
    got_rows, got_examples, got_counts = in_one_piece(
        (slot_rows, slot_examples, slot_counts), ROWS, 1, 0, 3
    )
    looked = lookup(got_rows[:, 0], tables)
    owner_examples = got_examples[:, 0]
    owner_live = slot_index[None, None, :] < got_counts[:, 0, :, None]
    source_count = examples_here * lax.axis_size(ROWS) // examples_here
    onehot = (
        (owner_examples[:, :, :, None] == example_ids[None, None, None, :])
        & owner_live[:, :, :, None]
    ).astype(jnp.float32)
    summed = jnp.einsum("stcb,stce->sbte", onehot, looked, precision=lax.Precision.HIGHEST)
    pooled = sum_by_axis(
        summed.reshape(source_count * examples_here, table_count, width),
        (("rows_0", "rows_1"), "rows_2"),
        0,
    )
    vectors = jnp.concatenate([dense_features[:, None, :], pooled], axis=1)
    gram_matrix = jnp.einsum("bie,bje->bij", vectors, vectors, precision=lax.Precision.HIGHEST)
    interactions = over_copies(upper_pairs(gram_matrix, table_count + 1) * E ** (-0.5), "cols")
    return (pooled, interactions)


def solution(mesh):
    torus = Mesh(
        mesh.devices.reshape(8, 4, 2, mesh.shape["cols"]), ("rows_0", "rows_1", "rows_2", "cols")
    )
    return jax.shard_map(
        body,
        mesh=torus,
        in_specs=(
            P(None, ROWS, "cols"),
            P(ROWS, "cols"),
            P(ROWS, None, None, None),
            P(ROWS, None, None, None),
            P(ROWS, None, None),
        ),
        out_specs=(P(ROWS, None, "cols"), P(ROWS, None)),
        check_vma=False,
    )
```

profile of v0, /device:TPU:2, one launch (start us, length us, event | category | flops | bytes accessed | tf_op | source)
XLA Modules:
  0.0 141.8 jit_solution(16277469829711478321)
XLA Ops:
  0.6 0.8 copy.40
  1.4 1.9 %pad_add_fusion = s32[1,64,4,129]{3,2,0,1:T(4,128)} fusion(s32[1,64,4,1]{3,2,0,1:T(4,128)S(1)} %copy.40, s32[1,64,4,64]{3,2,0,1:T(4,128)} %bitcast.50, s32[1,64,4,64]{3,2,0,1:T(4,128)} %bitcast.51), kind=kLoop, calls=%fused_computation.16 | loop fusion | flops 66048 | bytes 264192 | tf_op jit(solution)/shard_map/concatenate | solution.py:15
  3.3 12.0 %all-to-all-start = ((s32[1,64,4,129]{3,2,0,1:T(4,128)}), s32[1,64,4,129]{3,2,0,1:T(4,128)S(1)}, u32[]{:S(2)}, u32[]{:S(2)}) async-start(s32[1,64,4,129]{3,2,0,1:T(4,128)} %pad_add_fusion), calls=%async_computation | async-start | bytes 524288 | tf_op jit(solution)/shard_map/all_to_all | solution.py:18
  15.4 12.2 %all-to-all-done = s32[1,64,4,129]{3,2,0,1:T(4,128)S(1)} async-done(((s32[1,64,4,129]{3,2,0,1:T(4,128)}), s32[1,64,4,129]{3,2,0,1:T(4,128)S(1)}, u32[]{:S(2)}, u32[]{:S(2)}) %all-to-all-start) | async-done | bytes 132128 | tf_op jit(solution)/shard_map/all_to_all | solution.py:18
  27.5 0.1 slice_bitcast_fusion
  27.7 0.1 copy.42
  27.8 0.1 copy.43
  27.9 0.2 iota_compare_fusion.5
  28.1 23.8 %while.11 = (s32[]{:T(128)}, f32[4,64,64,128]{3,2,1,0:T(8,128)}, s32[4,64,64]{2,0,1:T(4,128)S(1)}, f32[4,512,128]{2,1,0:T(8,128)}, s32[]{:T(128)}) while((s32[]{:T(128)}, f32[4,64,64,128]{3,2,1,0:T(8,128)}, s32[4,64,64]{2,0,1:T(4,128)S(1)}, f32[4,512,128]{2,1,0:T(8,128)}, s32[]{:T(128)}) %tuple.29), condition=%wide.region_1.2_spmd.clone, body=%wide.region_0.1_spmd.clone.sunk | while | flops 3223322624 | bytes 2409545 | solution.py:62
  28.1 5.9 %bitcast_dynamic-update-slice_fusion.2 = f32[4,64,64,128]{3,2,1,0:T(8,128)} fusion(f32[4,64,64,128]{3,2,1,0:T(8,128)} %get-tuple-element.91, s32[]{:T(128)S(6)} %copy.61, s32[64,64]{1,0:T(8,128)S(1)} %bitcast.49, f32[4,512,128]{2,1,0:T(8,128)} %get-tuple-element.98), kind=kOutput, calls=%fused_computation.4.clone.1 | convolution fusion | flops 3223322624 | bytes 2376704 | tf_op jit(solution)/shard_map/while/body/eval_jaxpr/scr,re->sce/dot_general | solution.py:60
  34.1 5.9 %bitcast_dynamic-update-slice_fusion.2 = f32[4,64,64,128]{3,2,1,0:T(8,128)} fusion(f32[4,64,64,128]{3,2,1,0:T(8,128)} %get-tuple-element.91, s32[]{:T(128)S(6)} %copy.61, s32[64,64]{1,0:T(8,128)S(1)} %bitcast.49, f32[4,512,128]{2,1,0:T(8,128)} %get-tuple-element.98), kind=kOutput, calls=%fused_computation.4.clone.1 | convolution fusion | flops 3223322624 | bytes 2376704 | tf_op jit(solution)/shard_map/while/body/eval_jaxpr/scr,re->sce/dot_general | solution.py:60
  40.0 5.9 %bitcast_dynamic-update-slice_fusion.2 = f32[4,64,64,128]{3,2,1,0:T(8,128)} fusion(f32[4,64,64,128]{3,2,1,0:T(8,128)} %get-tuple-element.91, s32[]{:T(128)S(6)} %copy.61, s32[64,64]{1,0:T(8,128)S(1)} %bitcast.49, f32[4,512,128]{2,1,0:T(8,128)} %get-tuple-element.98), kind=kOutput, calls=%fused_computation.4.clone.1 | convolution fusion | flops 3223322624 | bytes 2376704 | tf_op jit(solution)/shard_map/while/body/eval_jaxpr/scr,re->sce/dot_general | solution.py:60
  45.9 5.9 %bitcast_dynamic-update-slice_fusion.2 = f32[4,64,64,128]{3,2,1,0:T(8,128)} fusion(f32[4,64,64,128]{3,2,1,0:T(8,128)} %get-tuple-element.91, s32[]{:T(128)S(6)} %copy.61, s32[64,64]{1,0:T(8,128)S(1)} %bitcast.49, f32[4,512,128]{2,1,0:T(8,128)} %get-tuple-element.98), kind=kOutput, calls=%fused_computation.4.clone.1 | convolution fusion | flops 3223322624 | bytes 2376704 | tf_op jit(solution)/shard_map/while/body/eval_jaxpr/scr,re->sce/dot_general | solution.py:60
  51.9 7.3 %fusion.7 = f32[64,4,128,32]{2,3,1,0:T(8,128)S(1)} fusion(s32[64,4,64]{2,1,0:T(4,128)S(1)} %get-tuple-element.58, pred[64,4,64]{2,1,0:T(4,128)(4,1)S(1)} %iota_compare_fusion.5, f32[4,64,64,128]{3,2,1,0:T(8,128)} %get-tuple-element.29), kind=kOutput, calls=%fused_computation.9 | convolution fusion | flops 806354944 | bytes 12664832 | tf_op jit(solution)/shard_map/stcb,stce->sbte/dot_general | solution.py:89
  59.1 0.8 copy.57
  59.9 8.2 %all_to_all.27 = f32[2,32,32,4,128]{4,2,3,1,0:T(8,128)} all-to-all(f32[2,32,32,4,128]{4,2,3,1,0:T(8,128)S(1)} %bitcast.46), channel_id=1, replica_groups=mesh['rows_0'=8,'rows_1'=4,'rows_2'=2,'cols'=4] {'rows_2'}, dimensions={0} | all-to-all | bytes 8388608 | tf_op jit(solution)/shard_map/all_to_all | solution.py:32
  68.1 0.0 copy-start.1
  68.1 2.9 %reduce_sum.27 = f32[32,32,4,128]{3,1,2,0:T(8,128)S(1)} reduce(f32[2,32,32,4,128]{4,2,3,1,0:T(8,128)} %all_to_all.27, f32[]{:T(128)} %constant.3.clone.1), dimensions={0}, to_apply=%region_2.3 | reduce | flops 524288 | bytes 6291460 | tf_op jit(solution)/shard_map/reduce_sum | solution.py:33
  71.0 56.0 %all_to_all.28 = f32[32,32,4,128]{3,1,2,0:T(8,128)} all-to-all(f32[32,32,4,128]{3,1,2,0:T(8,128)S(1)} %reduce_sum.27), channel_id=1, replica_groups=mesh['rows_0'=8,'rows_1'=4,'rows_2'=2,'cols'=4] {'rows_0','rows_1'}, dimensions={0} | all-to-all | bytes 4194304 | tf_op jit(solution)/shard_map/all_to_all | solution.py:40
  127.0 1.7 %reduce_sum.28 = f32[32,4,128]{2,0,1:T(8,128)S(1)} reduce(f32[32,32,4,128]{3,1,2,0:T(8,128)} %all_to_all.28, f32[]{:T(128)} %constant.3.clone.1), dimensions={0}, to_apply=%region_3.4 | reduce | flops 507904 | bytes 2162692 | tf_op jit(solution)/shard_map/reduce_sum | solution.py:41
  128.8 0.0 copy-start
  128.8 0.0 copy-done.1
  128.8 0.3 fusion.13
  129.2 0.5 slice_reduce_fusion
  129.6 0.1 slice.18
  129.8 0.1 slice.17
  129.9 0.1 slice.16
  130.0 0.1 copy.50
  130.0 0.1 copy.49
  130.1 0.1 copy.48
  130.2 0.1 reshape.21
  130.3 9.6 %all_to_all.29 = f32[4,1,320]{2,1,0:T(1,128)S(1)} all-to-all(f32[4,1,320]{2,1,0:T(1,128)S(1)} %reshape.21), channel_id=1, replica_groups=mesh['rows_0'=8,'rows_1'=4,'rows_2'=2,'cols'=4] {'cols'}, dimensions={0} | all-to-all | bytes 10240 | tf_op jit(solution)/shard_map/all_to_all | solution.py:46
  139.9 0.5 broadcast.7
  140.4 0.7 reduce.2
  141.1 0.1 reshape.22
  141.2 0.6 bitcast_reduce_fusion
  141.8 0.0 copy-done
  (9 shorter events, 0.2 us)
Async XLA Ops:
  3.3 24.2 %all-to-all-start = ((s32[1,64,4,129]{3,2,0,1:T(4,128)}), s32[1,64,4,129]{3,2,0,1:T(4,128)S(1)}, u32[]{:S(2)}, u32[]{:S(2)}) async-start(s32[1,64,4,129]{3,2,0,1:T(4,128)} %pad_add_fusion), calls=%async_computation | async-start | bytes 524288 | tf_op jit(solution)/shard_map/all_to_all | solution.py:18
  68.1 60.7 %copy-start.1 = (f32[32,128]{1,0:T(8,128)S(1)}, f32[32,128]{1,0:T(8,128)}, u32[]{:S(2)}) copy-start(f32[32,128]{1,0:T(8,128)} %param.8) | copy-start | bytes 49156
  128.8 13.0 %copy-start = (f32[32,4,128]{2,1,0:T(4,128)}, f32[32,4,128]{2,1,0:T(4,128)S(1)}, u32[]{:S(2)}) copy-start(f32[32,4,128]{2,1,0:T(4,128)S(1)} %copy.51) | copy-start | bytes 196612
where the time goes:
time: 142 us
  blocking collectives  73.7 us (52%)
  matrix products  31.3 us (22%)
  waiting for transfers between devices  12.2 us (9%)
  starting transfers between devices  12 us (8%)
  other arithmetic  7.95 us (6%)
  local copies, waits for them, and re-layouts  3.82 us (3%)
    all_to_all x1, blocking collectives, sum_by_axis(): lax.all_to_all(nearer, far, split_axis=0, concat_axis=0, tiled=True)  56 us
    dot_general x4, matrix products, one_table(): jnp.einsum('scr,re->sce', selector, table_slice, precision=lax.Precision....  23.6 us
    all_to_all x1, waiting for transfers between devices, in_one_piece(): lax.all_to_all(both, axis, split_axis=split_dim, concat_axis=concat_dim,...  12.2 us
    all_to_all x1, starting transfers between devices, in_one_piece(): lax.all_to_all(both, axis, split_axis=split_dim, concat_axis=concat_dim,...  12 us
    all_to_all x1, blocking collectives, copy_for_each(): return lax.all_to_all(copies, axis, split_axis=0, concat_axis=0, tiled=True)  9.56 us
    all_to_all x1, blocking collectives, sent_and_summed(): tiles = lax.all_to_all(in_blocks(x, dim, size), axis, 0, 0, tiled=True)  8.17 us
    dot_general x1, matrix products, body(): jnp.einsum('stcb,stce->sbte', onehot, looked, precision=lax.Precision.HIG...  7.26 us
    reduce_sum x1, other arithmetic, sent_and_summed(): return jnp.sum(tiles, axis=0)  2.88 us
  transfers between devices with their start and end apart: 1, of which 1 were waited for; matrix products, arithmetic and copies ran while one was open for 0% of the time, Pallas kernels for 0%

commit v1 on v0

v1 whole, which is shorter than its diff:
```python
import functools

import jax
import jax.numpy as jnp
from jax import lax
from jax.experimental import pallas as pl
from jax.experimental.pallas import tpu as pltpu
from jax.sharding import PartitionSpec as P

E = 512
NX, NZ, NY = 4, 8, 4
TABLES = 4
ROWS_DEV = 512
B = 32
CAP = 64
W = 128
HALF_ROWS = 256
RA = 64
RB = TABLES * B - RA
N_SEM = 128
MESH = pl.DeviceIdType.MESH
F32 = jnp.float32
BF16 = jnp.bfloat16


def kernel(
    tables, dense, rows_in, ex_in, counts,
    pooled_out, inter_out,
    rows_v, ex_v, cnt_v, dense_v, tab_own, tab_oth, tb, msg, r1, r2, mb, part,
    xr, xl, xm, sa, zra, zla, zsra, zsla, zrb, zlb, zsrb, zslb, sb, bxr, bxl, bxm, fin,
    ybuf, yin, lsem, ssem, rsem,
):
    me = lax.axis_index("rows")
    y = lax.axis_index("cols")
    core = lax.rem(me, 2)
    chip = lax.div(me, 2)
    x = lax.rem(chip, NX)
    z = lax.div(chip, NX)

    def dev(dz=0, dx=0, dy=0, dc=0):
        zz = lax.rem(z + dz, NZ)
        xx = lax.rem(x + dx, NX)
        cc = lax.rem(core + dc, 2)
        return ((zz * NX + xx) * 2 + cc, lax.rem(y + dy, NY))

    used = []

    def send(src, dst, to):
        i = len(used)
        copy = pltpu.make_async_remote_copy(
            src_ref=src, dst_ref=dst, send_sem=ssem.at[i], recv_sem=rsem.at[i],
            device_id=to, device_id_type=MESH,
        )
        copy.start()
        used.append(copy)
        return copy

    locals_ = [
        pltpu.make_async_copy(rows_in, rows_v, lsem.at[0]),
        pltpu.make_async_copy(ex_in, ex_v, lsem.at[1]),
        pltpu.make_async_copy(counts, cnt_v, lsem.at[2]),
        pltpu.make_async_copy(tables, tab_own, lsem.at[3]),
        pltpu.make_async_copy(dense, dense_v, lsem.at[4]),
    ]
    for c in locals_:
        c.start()

    barrier = pltpu.get_barrier_semaphore()
    peers = [dev(dz=d) for d in range(1, NZ)] + [dev(dx=d) for d in range(1, NX)]
    peers += [dev(dy=d) for d in range(1, NY)] + [dev(dc=1)]
    for p in peers:
        pl.semaphore_signal(barrier, inc=1, device_id=p, device_id_type=MESH)

    for c in locals_[:3]:
        c.wait()
    lane = lax.broadcasted_iota(jnp.int32, (TABLES, W), 1)
    first = lane < CAP
    swap = core == 1
    for j in range(NX * NZ):
        own_r, oth_r = rows_v[j, core], rows_v[j, 1 - core]
        own_e, oth_e = ex_v[j, core], ex_v[j, 1 - core]
        even = jnp.broadcast_to(cnt_v[:, 2 * j : 2 * j + 1], (TABLES, W))
        odd = jnp.broadcast_to(cnt_v[:, 2 * j + 1 : 2 * j + 2], (TABLES, W))
        own_c = jnp.where(swap, odd, even)
        oth_c = jnp.where(swap, even, odd)
        bound = jnp.where(first, own_c, oth_c + CAP)
        ex = jnp.where(lane < bound, jnp.concatenate([own_e, oth_e], axis=1), -1)
        msg[j // NX, j % NX, 0:TABLES] = jnp.concatenate([own_r, oth_r], axis=1)
        msg[j // NX, j % NX, TABLES : 2 * TABLES] = ex

    pl.semaphore_wait(barrier, len(peers))

    ids_x = {}
    for j in (2, 1, 3):
        ids_x[j] = send(msg.at[:, lax.rem(x + j, NX)], r1.at[NX - j - 1], dev(dx=j))
    ids_z0 = {}
    for d in (4, 3, 5, 2, 6, 1, 7):
        ids_z0[d] = send(msg.at[lax.rem(z + d, NZ), x], r2.at[NZ - d, 0], dev(dz=d))
    tab_copy = send(tables, tab_oth, dev(dc=1))

    def split(src, half):
        for t in range(TABLES):
            v = src[t]
            hi = v.astype(BF16)
            lo = (v - hi.astype(F32)).astype(BF16)
            tb[t, half * ROWS_DEV : (half + 1) * ROWS_DEV, 0:W] = hi
            tb[t, half * ROWS_DEV : (half + 1) * ROWS_DEV, W : 2 * W] = lo

    locals_[3].wait()
    split(tab_own, 0)
    for j in (1, 2, 3):
        ids_x[j].wait_recv()
    ids_z1 = {}
    for d in (4, 3, 5, 2, 6, 1, 7):
        ids_z1[d] = send(r1.at[:, lax.rem(z + d, NZ)], r2.at[NZ - d, pl.ds(1, NX - 1)], dev(dz=d))
    tab_copy.wait_recv()
    split(tab_oth, 1)

    iota_a = lax.broadcasted_iota(jnp.int32, (W, W), 0)
    iota_b = lax.broadcasted_iota(jnp.int32, (HALF_ROWS, W), 0)
    core_key = jnp.where(first, 0, 2 * B)
    nt = (((1,), (1,)), ((), ()))

    def compute(zi):
        if zi:
            ids_z0[NZ - zi].wait_recv()
            ids_z1[NZ - zi].wait_recv()
        for s in range(NX):
            if zi:
                rows4, ex4 = r2[zi, s, 0:TABLES], r2[zi, s, TABLES : 2 * TABLES]
            elif s:
                rows4, ex4 = r1[s - 1, z, 0:TABLES], r1[s - 1, z, TABLES : 2 * TABLES]
            else:
                rows4, ex4 = msg[z, x, 0:TABLES], msg[z, x, TABLES : 2 * TABLES]
            key4 = jnp.where(ex4 >= 0, core_key + lax.shift_left(lax.shift_right_logical(rows4, 8), 5) + ex4, -1)
            low4 = rows4 & (HALF_ROWS - 1)
            for t in range(TABLES):
                a = jnp.where(iota_a == key4[t : t + 1], 1.0, 0.0).astype(BF16)
                b = jnp.where(iota_b == low4[t : t + 1], 1.0, 0.0).astype(BF16)
                m = lax.dot_general(a, b, nt, preferred_element_type=F32).astype(BF16)
                for q in range(4):
                    mb[t, s * B : (s + 1) * B, q * HALF_ROWS : (q + 1) * HALF_ROWS] = m[q * B : (q + 1) * B]
        for t in range(TABLES):
            o = jnp.dot(mb[t], tb[t], preferred_element_type=F32)
            o = o[:, 0:W] + o[:, W : 2 * W]
            for s in range(NX):
                part[zi, s, t * B : (t + 1) * B] = o[s * B : (s + 1) * B]

    class XPhase:
        def __init__(self, src, n, r, l, m):
            self.src, self.h, self.r, self.l, self.m = src, n // 2, r, l, m

        def piece(self, j, half):
            return self.src(j).at[pl.ds(half * self.h, self.h)]

        def start(self):
            self.r0 = send(self.piece(2, 0), self.r.at[0], dev(dx=1))
            self.l0 = send(self.piece(2, 1), self.l.at[0], dev(dx=NX - 1))
            self.r1 = send(self.piece(1, 1), self.r.at[1], dev(dx=1))
            self.l1 = send(self.piece(3, 0), self.l.at[1], dev(dx=NX - 1))

        def middle(self):
            self.r0.wait_recv()
            self.m[0] = self.r[0] + self.piece(1, 0)[...]
            self.r2 = send(self.m.at[0], self.r.at[2], dev(dx=1))
            self.l0.wait_recv()
            self.m[1] = self.l[0] + self.piece(3, 1)[...]
            self.l2 = send(self.m.at[1], self.l.at[2], dev(dx=NX - 1))

        def finish(self, out):
            for c in (self.r1, self.l1, self.r2, self.l2):
                c.wait_recv()
            out[0 : self.h] = self.piece(0, 0)[...] + self.l[1] + self.r[2]
            out[self.h : 2 * self.h] = self.piece(0, 1)[...] + self.r[1] + self.l[2]

    class ZPhase:
        def __init__(self, src, n, r, l, sr, sl):
            self.src, self.n, self.h = src, n, n // 2
            self.r, self.l, self.sr, self.sl = r, l, sr, sl
            self.cr, self.cl = {}, {}

        def step0(self):
            h = self.h
            self.cr[0] = send(self.src(4).at[pl.ds(0, h)], self.r(0).at[pl.ds(0, h)], dev(dz=1))
            self.cl[0] = send(self.src(4).at[pl.ds(h, h)], self.l(0).at[pl.ds(h, h)], dev(dz=NZ - 1))

        def step(self, k):
            h = self.h
            a, b = self.src(4 - k), self.src(4 + k)
            self.cr[k - 1].wait_recv()
            self.sr(k)[0:h] = self.r(k - 1)[0:h] + a[0:h]
            self.sr(k)[h:] = a[h:] if k == 1 else self.r(k - 1)[h:] + a[h:]
            self.cr[k] = send(self.sr(k), self.r(k), dev(dz=1))
            self.cl[k - 1].wait_recv()
            self.sl(k)[h:] = self.l(k - 1)[h:] + b[h:]
            self.sl(k)[0:h] = b[0:h] if k == 1 else self.l(k - 1)[0:h] + b[0:h]
            self.cl[k] = send(self.sl(k), self.l(k), dev(dz=NZ - 1))

        def finish(self, out):
            self.cr[3].wait_recv()
            self.cl[3].wait_recv()
            out[...] = self.src(0)[...] + self.r(3)[...] + self.l(3)[...]

    ax = [
        XPhase(lambda j, k=k: part.at[k, j, pl.ds(0, RA)], RA, xr.at[k], xl.at[k], xm.at[k])
        for k in range(NZ)
    ]
    az = ZPhase(
        lambda k: sa.at[k % NZ], RA, lambda k: zra.at[k], lambda k: zla.at[k],
        lambda k: zsra.at[k - 1], lambda k: zsla.at[k - 1],
    )
    bz = [
        ZPhase(
            lambda k, j=j: part.at[k % NZ, j, pl.ds(RA, RB)], RB,
            lambda k, j=j: zrb.at[k, j], lambda k, j=j: zlb.at[k, j],
            lambda k, j=j: zsrb.at[k - 1, j], lambda k, j=j: zslb.at[k - 1, j],
        )
        for j in range(NX)
    ]
    bx = XPhase(lambda j: sb.at[j], RB, bxr, bxl, bxm)
    order_j = (2, 1, 3, 0)

    def bstep(k):
        for j in order_j:
            bz[j].step(k)

    compute(0)
    ax[0].start()
    compute(4)
    for j in order_j:
        bz[j].step0()
    ax[4].start()
    ax[0].middle()
    compute(3)
    ax[3].start()
    compute(5)
    ax[5].start()
    ax[4].middle()
    ax[0].finish(sa.at[0])
    bstep(1)
    compute(2)
    ax[2].start()
    ax[3].middle()
    ax[5].middle()
    ax[4].finish(sa.at[4])
    az.step0()
    compute(6)
    ax[6].start()
    ax[2].middle()
    ax[3].finish(sa.at[3])
    ax[5].finish(sa.at[5])
    bstep(2)
    az.step(1)
    compute(1)
    ax[1].start()
    ax[6].middle()
    ax[2].finish(sa.at[2])
    compute(7)
    ax[7].start()
    ax[1].middle()
    ax[6].finish(sa.at[6])
    bstep(3)
    az.step(2)
    ax[7].middle()
    ax[1].finish(sa.at[1])
    ax[7].finish(sa.at[7])
    az.step(3)
    for j in order_j:
        bz[j].finish(sb.at[j])
    bx.start()
    bx.middle()
    az.finish(fin.at[pl.ds(0, RA)])
    bx.finish(fin.at[pl.ds(RA, RB)])

    locals_[4].wait()
    vec = [dense_v[...]] + [fin[t * B : (t + 1) * B] for t in range(TABLES)]
    for t in range(TABLES):
        pooled_out[:, t, :] = vec[1 + t]
    prods = [vec[i] * vec[j] for i in range(TABLES + 1) for j in range(i + 1, TABLES + 1)]
    prods += [jnp.zeros_like(prods[0])] * 2
    sums = []
    for g in range(3):
        stacked = jnp.concatenate(prods[4 * g : 4 * g + 4], axis=0)
        sums.append(jnp.sum(stacked.T, axis=0, keepdims=True))
    ybuf[...] = jnp.concatenate(sums + [jnp.zeros((5, W), F32)], axis=0)
    ycopies = [send(ybuf, yin.at[NY - j - 1], dev(dy=j)) for j in (2, 1, 3)]
    for c in ycopies:
        c.wait_recv()
    total = (ybuf[...] + yin[0] + yin[1] + yin[2]) * (E ** -0.5)
    for p in range(10):
        inter_out[p : p + 1, :] = total[p // 4 : p // 4 + 1, (p % 4) * B : (p % 4 + 1) * B]
    for c in used:
        c.wait_send()


def body(tables, dense, slot_rows, slot_examples, slot_counts):
    any_ = pl.BlockSpec(memory_space=pl.ANY)
    vmem = pl.BlockSpec(memory_space=pltpu.VMEM)
    V = pltpu.VMEM
    HA, HB = RA // 2, RB // 2
    scratch = [
        V((NX * NZ, 2, TABLES, CAP), jnp.int32),
        V((NX * NZ, 2, TABLES, CAP), jnp.int32),
        V((TABLES, 2 * NX * NZ), jnp.int32),
        V((B, W), F32),
        V((TABLES, ROWS_DEV, W), F32),
        V((TABLES, ROWS_DEV, W), F32),
        V((TABLES, 2 * ROWS_DEV, 2 * W), BF16),
        V((NZ, NX, 8, W), jnp.int32),
        V((NX - 1, NZ, 8, W), jnp.int32),
        V((NZ, NX, 8, W), jnp.int32),
        V((TABLES, W, 4 * HALF_ROWS), BF16),
        V((NZ, NX, TABLES * B, W), F32),
        V((NZ, 3, HA, W), F32),
        V((NZ, 3, HA, W), F32),
        V((NZ, 2, HA, W), F32),
        V((NZ, RA, W), F32),
        V((4, RA, W), F32),
        V((4, RA, W), F32),
        V((3, RA, W), F32),
        V((3, RA, W), F32),
        V((4, NX, RB, W), F32),
        V((4, NX, RB, W), F32),
        V((3, NX, RB, W), F32),
        V((3, NX, RB, W), F32),
        V((NX, RB, W), F32),
        V((3, HB, W), F32),
        V((3, HB, W), F32),
        V((2, HB, W), F32),
        V((TABLES * B, W), F32),
        V((8, W), F32),
        V((NY - 1, 8, W), F32),
        pltpu.SemaphoreType.DMA((5,)),
        pltpu.SemaphoreType.DMA((N_SEM,)),
        pltpu.SemaphoreType.DMA((N_SEM,)),
    ]
    pooled, inter = pl.pallas_call(
        kernel,
        out_shape=(
            jax.ShapeDtypeStruct((B, TABLES, W), F32),
            jax.ShapeDtypeStruct((10, B), F32),
        ),
        in_specs=[any_] * 5,
        out_specs=(vmem, vmem),
        scratch_shapes=scratch,
        compiler_params=pltpu.CompilerParams(
            collective_id=0, has_side_effects=True, vmem_limit_bytes=56 * 1024 * 1024
        ),
    )(
        tables,
        dense,
        slot_rows.reshape(NX * NZ, 2, TABLES, CAP),
        slot_examples.reshape(NX * NZ, 2, TABLES, CAP),
        slot_counts[0].T,
    )
    return pooled, inter.T


def solution(mesh):
    return jax.shard_map(
        body,
        mesh=mesh,
        in_specs=(
            P(None, "rows", "cols"),
            P("rows", "cols"),
            P("rows", None, None, None),
            P("rows", None, None, None),
            P("rows", None, None),
        ),
        out_specs=(P("rows", None, "cols"), P("rows", None)),
        check_vma=False,
    )
```

time: 142 us -> 53.7 us (0.38)
  blocking collectives: 73.7 us -> 0 us
  Pallas kernels: 0 us -> 50.9 us
  matrix products: 31.3 us -> 0 us
  waiting for transfers between devices: 12.2 us -> 0 us
  starting transfers between devices: 12 us -> 0 us
  other arithmetic: 7.95 us -> 0 us
  local copies, waits for them, and re-layouts: 3.82 us -> 2.08 us
    all_to_all x3 -> x0, blocking collectives: 73.7 us -> none  [the longest x1 56 us: sum_by_axis(): lax.all_to_all(nearer, far, split_axis=0, concat_axis=0, tiled=True)]
    pallas_call x0 -> x1, Pallas kernels: none -> 50.9 us  [body(): pl.pallas_call(kernel, out_shape=(jax.ShapeDtypeStruct((B, TABLES, W), F3...]
    dot_general x6 -> x0, matrix products: 31.3 us -> none  [the longest x4 23.6 us: one_table(): jnp.einsum('scr,re->sce', selector, table_slice, precision=lax.Precision....]
    all_to_all x1 -> x0, waiting for transfers between devices: 12.2 us -> none  [in_one_piece(): lax.all_to_all(both, axis, split_axis=split_dim, concat_axis=concat_dim,...]
    all_to_all x1 -> x0, starting transfers between devices: 12 us -> none  [in_one_piece(): lax.all_to_all(both, axis, split_axis=split_dim, concat_axis=concat_dim,...]
    reduce_sum x3 -> x0, other arithmetic: 5.22 us -> none  [the longest x1 2.88 us: sent_and_summed(): return jnp.sum(tiles, axis=0)]
    concatenate x1 -> x0, other arithmetic: 1.88 us -> none  [in_one_piece(): jnp.concatenate([a.reshape(*a.shape[:along], w) for a, w in zip(arrays, w...]
    unnamed x8 -> x4, local copies, waits for them, and re-layouts: 0.23 us -> 2.08 us
  transfers between devices with their start and end apart: 1 -> 0, of which waited for: 1 -> 0; matrix products, arithmetic and copies ran while one was open for 0% -> 0% of each run, Pallas kernels for 0% -> 0%
where the time goes in v1:
time: 53.7 us; the launch traced here: 53.6 us
  Pallas kernels  50.9 us (95%)
  local copies, waits for them, and re-layouts  2.08 us (4%)
  between operations  0.65 us (1%)
    pallas_call x1, Pallas kernels, body(): pl.pallas_call(kernel, out_shape=(jax.ShapeDtypeStruct((B, TABLES, W), F3...  50.9 us
    unnamed x4, local copies, waits for them, and re-layouts  2.08 us

profile of v1, /device:TPU:2, one launch (start us, length us, event | category | flops | bytes accessed | tf_op | source)
XLA Modules:
  0.0 53.6 jit_solution(920016708283142463)
XLA Ops:
  0.6 50.9 %shard_map.68 = (f32[32,4,128]{2,1,0:T(4,128)}, f32[10,32]{1,0:T(8,128)}) custom-call(f32[4,512,128]{2,1,0:T(8,128)} %tables.1, f32[32,128]{1,0:T(8,128)} %dense.1, s32[32,2,4,64]{3,2,1,0:T(4,128)} %bitcast.6, s32[32,2,4,64]{3,2,1,0:T(4,128)} %bitcast.7, s32[4,64]{1,0:T(4,128)} %bitcast.9), custom_call_target="tpu_custom_call" | custom-call | tf_op jit(solution)/shard_map/pallas_call | solution.py:337
  51.5 0.0 copy-start
  51.5 1.5 %copy.9 = f32[32,4,128]{2,1,0:T(4,128)} copy(f32[32,4,128]{2,1,0:T(4,128)} %get-tuple-element.8) | data formatting | bytes 131072
  53.0 0.0 copy-done
  53.0 0.6 %copy.10 = f32[32,10]{0,1:T(8,128)} copy(f32[32,10]{0,1:T(8,128)S(1)} %bitcast.8) | data formatting | bytes 2560
Async XLA Ops:
  51.5 1.5 %copy-start = (f32[10,32]{1,0:T(8,128)S(1)}, f32[10,32]{1,0:T(8,128)}, u32[]{:S(2)}) copy-start(f32[10,32]{1,0:T(8,128)} %get-tuple-element.5) | copy-start | bytes 3844
